TPU v7x, 256 devices: a whole 4x4x8 slice. The times are simulated.
256 devices in a mesh: row: 4 (over y_lo, core), col: 64 (over z, y_hi, x).
Axes of the slice: x: 4, y: 4 (y_hi: 2, y_lo: 2; y = y_hi * 2 + y_lo), z: 8, core: 2. Of those that a mesh axis runs over, the one named last changes fastest.
Arguments:
- image: bfloat16 [8192, 1024], P(('col', 'row')), may hold values from -1 to 1
- text: bfloat16 [8192, 1024], P(('row', 'col')), may hold values from -1 to 1
- audio: bfloat16 [8192, 1024], P(('row', 'col')), may hold values from -1 to 1
Outputs:
- image_grad: float32 [8192, 1024], P(('col', 'row'))
- text_grad: float32 [8192, 1024], P(('row', 'col'))
- audio_grad: float32 [8192, 1024], P(('row', 'col'))
- loss: float32 [], replicated
All inputs are finite; a program needn't handle non-finite values.
Results may differ from a plain program's by a relative error of at most 0.0063.
Values may be sent and summed in bfloat16 or wider, within the bound.
No kernel may reach another device: no remote copies, remote signals or barrier semaphores. Data moves between devices by JAX's collectives and lax.ppermute only.
A program may use at most 64 MiB of HBM per device.

v0:
```python
import functools
import jax
import jax.numpy as jnp
from jax import lax
from jax.sharding import Mesh
from jax.sharding import PartitionSpec as P

ROW = ("row_0", "row_1")
COL = ("col_0", "col_1", "col_2")
ROW_COL = ("row_0", "row_1", "col_0", "col_1", "col_2")
COL_ROW = ("col_0", "col_1", "col_2", "row_0", "row_1")
logit_scale = 20.0
epsilon = 1e-06


def joined_along(parts, dim):
    lengths = list(parts.shape[1:])
    lengths[dim] *= parts.shape[0]
    return jnp.moveaxis(parts, 0, dim).reshape(lengths)


def stacked_from(array, axes, sequence):
    parts = array[None]
    for k in sequence:
        parts = lax.all_gather(parts, axes[k], axis=0, tiled=True)
    carried = [lax.axis_size(axes[k]) for k in reversed(sequence)]
    parts = parts.reshape(*carried, *array.shape)
    turned = sorted(range(len(sequence)), key=lambda place: sequence[len(sequence) - 1 - place])
    return parts.transpose(*turned, *range(len(sequence), parts.ndim)).reshape(-1, *array.shape)


def gather_axes(array, axes, sequence, dim):
    return joined_along(stacked_from(array, axes, sequence), dim)


def side_by_side(arrays, axis, dim, along):
    ends, at = ([], 0)
    for a in arrays[:-1]:
        at += a.shape[along]
        ends.append(at)
    both = jnp.concatenate(arrays, axis=along)
    return tuple(jnp.split(lax.all_gather(both, axis, axis=dim, tiled=True), ends, axis=along))


def copy_for_each(array, axis):
    copies = jnp.broadcast_to(array, (lax.axis_size(axis), *array.shape))
    return lax.all_to_all(copies, axis, split_axis=0, concat_axis=0, tiled=True)


def of_everyone(array, axis):
    return copy_for_each(array, axis).sum(axis=0)


def in_one(arrays, axis):
    ends = [0]
    for a in arrays:
        ends.append(ends[-1] + a.size)
    total = of_everyone(jnp.concatenate([a.ravel() for a in arrays]), axis)
    return tuple((total[b:e].reshape(a.shape) for a, b, e in zip(arrays, ends, ends[1:])))


def split_up(array, dim, peers):
    lengths = array.shape
    parts = array.reshape(*lengths[:dim], peers, lengths[dim] // peers, *lengths[dim + 1 :])
    return jnp.moveaxis(parts, dim, 0)


def summed_on_arrival(array, axis, dim):
    peers = lax.axis_size(axis)
    parts = lax.all_to_all(split_up(array, dim, peers), axis, 0, 0, tiled=True)
    return jnp.sum(parts.astype(jnp.float32), axis=0)


def sum_by_axis(array, axes, dim):
    far, near = axes
    parts = split_up(array, dim, lax.axis_size(far))
    nearer = summed_on_arrival(parts, near, dim + 1)
    arrived = lax.all_to_all(
        nearer.astype(jnp.bfloat16), far, split_axis=0, concat_axis=0, tiled=True
    )
    return arrived.astype(jnp.float32).sum(axis=0)


def over_axes(array, axes):
    return functools.reduce(lax.psum, axes, array)


def normalize(values):
    widened = values.astype(jnp.float32)
    radius = jnp.sqrt(jnp.sum(widened * widened, axis=-1, keepdims=True) + epsilon)
    return (widened / radius, radius)


def through_norm(grad_unit, unit, radius):
    inner = jnp.sum(unit * grad_unit, axis=-1, keepdims=True)
    return (grad_unit - unit * inner) / radius


def scores(left, right):
    return logit_scale * lax.dot_general(
        left, right, (((1,), (1,)), ((), ())), preferred_element_type=jnp.float32
    )


def contract_rows(weights_part, image_tile):
    return lax.dot_general(
        weights_part, image_tile, (((0,), (0,)), ((), ())), preferred_element_type=jnp.float32
    )


def pair_scores(image_tile, text_tile, audio_tile):
    text_scores = scores(image_tile, text_tile)
    audio_scores = scores(image_tile, audio_tile)
    return (
        text_scores,
        audio_scores,
        jnp.exp(text_scores - logit_scale),
        jnp.exp(audio_scores - logit_scale),
    )


def softmax_weights(exp_tile, row_total, column_total, twice_diagonal):
    return (
        exp_tile / row_total[:, None] + exp_tile / column_total[None, :] - twice_diagonal
    ).astype(jnp.bfloat16)


def own_logs(totals, first_row, amount):
    return jnp.sum(jnp.log(lax.dynamic_slice_in_dim(totals, first_row, amount, 0)))


def shards(image, text, audio):
    rows_here = image.shape[0]
    feature_width = image.shape[1]
    image_unit, image_radius = normalize(image)
    text_unit, text_radius = normalize(text)
    audio_unit, audio_radius = normalize(audio)
    image_half = image_unit.astype(jnp.bfloat16)
    text_half = text_unit.astype(jnp.bfloat16)
    audio_half = audio_unit.astype(jnp.bfloat16)
    row_place = lax.axis_index(ROW)
    col_place = lax.axis_index(COL)
    row_count = lax.axis_size(ROW)
    col_count = lax.axis_size(COL)
    image_tile = gather_axes(image_half, COL, (1, 0, 2), 0)
    text_tile, audio_tile = side_by_side((text_half, audio_half), ROW, 0, 1)
    image_local = jnp.arange(col_count * rows_here, dtype=jnp.int32)
    image_ids = (
        image_local // rows_here * row_count + row_place
    ) * rows_here + image_local % rows_here
    pair_local = jnp.arange(row_count * rows_here, dtype=jnp.int32)
    pair_ids = (
        pair_local // rows_here * col_count + col_place
    ) * rows_here + pair_local % rows_here
    text_scores, audio_scores, text_exp, audio_exp = pair_scores(image_tile, text_tile, audio_tile)
    text_row, audio_row = in_one((jnp.sum(text_exp, axis=1), jnp.sum(audio_exp, axis=1)), COL)
    text_column, audio_column = in_one((jnp.sum(text_exp, axis=0), jnp.sum(audio_exp, axis=0)), ROW)
    diagonal = image_ids[:, None] == pair_ids[None, :]
    twice_diagonal = jnp.where(diagonal, 2.0, 0.0).astype(jnp.float32)
    text_weights = softmax_weights(text_exp, text_row, text_column, twice_diagonal)
    audio_weights = softmax_weights(audio_exp, audio_row, audio_column, twice_diagonal)
    image_part = logit_scale * sum_by_axis(
        (
            jnp.dot(text_weights, text_tile, preferred_element_type=jnp.float32)
            + jnp.dot(audio_weights, audio_tile, preferred_element_type=jnp.float32)
        ).astype(jnp.bfloat16),
        (("col_0", "col_1"), "col_2"),
        0,
    )
    partial_value = jnp.concatenate(
        [contract_rows(text_weights, image_tile), contract_rows(audio_weights, image_tile)], axis=1
    )
    pair_part = logit_scale * summed_on_arrival(partial_value.astype(jnp.bfloat16), ROW, 0)
    image_first = col_place * rows_here
    pair_first = row_place * rows_here
    loss_part = (
        own_logs(text_row, image_first, rows_here)
        + own_logs(audio_row, image_first, rows_here)
        + own_logs(text_column, pair_first, rows_here)
        + own_logs(audio_column, pair_first, rows_here)
        - 2.0 * jnp.sum(jnp.where(diagonal, text_scores + audio_scores, 0.0))
    )
    batch_size = rows_here * row_count * col_count
    loss = over_axes(loss_part, ROW_COL) / (4.0 * batch_size) + logit_scale
    return (
        through_norm(image_part, image_unit, image_radius),
        through_norm(pair_part[:, :feature_width], text_unit, text_radius),
        through_norm(pair_part[:, feature_width:], audio_unit, audio_radius),
        loss,
    )


def solution(mesh):
    split = Mesh(mesh.devices.reshape(2, 2, 8, 2, 4), ("row_0", "row_1", "col_0", "col_1", "col_2"))
    placed = (P(COL_ROW, None), P(ROW_COL, None), P(ROW_COL, None))
    return jax.shard_map(
        shards,
        mesh=split,
        in_specs=placed,
        out_specs=(P(COL_ROW, None), P(ROW_COL, None), P(ROW_COL, None), P()),
        check_vma=False,
    )
```

profile of v0, /device:TPU:24, one launch (start us, length us, event | category | flops | bytes accessed | tf_op | source)
XLA Modules:
  0.0 305.4 jit_solution(18293533622989130421)
XLA Ops:
  7.2 1.0 fusion.24
  8.2 0.9 fusion.46
  9.1 6.5 %all-gather = bf16[64,1024]{1,0:T(8,128)(2,1)} all-gather(bf16[32,1024]{1,0:T(8,128)(2,1)S(1)} %fusion.46), channel_id=2, replica_groups=mesh['row_0'=2,'row_1'=2,'col_0'=8,'col_1'=2,'col_2'=4] {'col_1'}, dimensions={0}, use_global_device_ids=true | all-gather | bytes 196608 | tf_op jit(solution)/shard_map/all_gather | solution.py:25
  15.7 0.0 all-gather.6.cloned.1.call-start
  15.7 41.2 %all-gather.4.cloned.1.call-done = bf16[16,32,1024]{2,1,0:T(8,128)(2,1)} async-done(((bf16[2,32,1024]{2,1,0:T(8,128)(2,1)}), bf16[16,32,1024]{2,1,0:T(8,128)(2,1)}) %all-gather.4.cloned.1.call-update) | async-done | bytes 1048592 | tf_op jit(solution)/shard_map/all_gather | solution.py:25
  57.0 1.0 fusion.25
  58.0 1.0 fusion.26
  59.0 1.0 fusion.47
  60.0 6.5 %all_gather.15 = bf16[128,2048]{1,0:T(8,128)(2,1)S(1)} all-gather(bf16[32,2048]{1,0:T(8,128)(2,1)S(1)} %pad_maximum_fusion.1), channel_id=1, replica_groups=mesh['row_0'=2,'row_1'=2,'col_0'=8,'col_1'=2,'col_2'=4] {'row_0','row_1'}, dimensions={0}, use_global_device_ids=true | all-gather | bytes 655360 | tf_op jit(solution)/shard_map/all_gather | solution.py:42
  66.5 41.4 %all-gather.6.cloned.1.call-done = bf16[64,32,1024]{2,1,0:T(8,128)(2,1)} async-done(((bf16[16,32,1024]{2,1,0:T(8,128)(2,1)}), bf16[64,32,1024]{2,1,0:T(8,128)(2,1)}) %all-gather.6.cloned.1.call-update) | async-done | bytes 4194320 | tf_op jit(solution)/shard_map/all_gather | solution.py:25
  107.9 2.6 copy.12
  110.6 1.5 convolution_multiply_fusion
  112.1 2.4 fusion
  114.5 0.6 broadcast_in_dim.37
  115.1 4.1 %all-to-all-start.1 = ((f32[4,1,256]{2,1,0:T(1,128)}), f32[4,1,256]{2,1,0:T(1,128)S(1)}, u32[]{:S(2)}, u32[]{:S(2)}) async-start(f32[4,1,256]{2,1,0:T(1,128)} %broadcast_in_dim.37), calls=%async_computation.1 | async-start | bytes 8192 | tf_op jit(solution)/shard_map/all_to_all | solution.py:47
  119.2 1.8 all-to-all-done.1
  121.0 2.0 broadcast_in_dim.36
  123.0 12.0 %all-to-all-start = ((f32[64,1,4096]{2,1,0:T(1,128)}), f32[64,1,4096]{2,1,0:T(1,128)S(1)}, u32[]{:S(2)}, u32[]{:S(2)}) async-start(f32[64,1,4096]{2,1,0:T(1,128)} %broadcast_in_dim.36), calls=%async_computation | async-start | bytes 2097152 | tf_op jit(solution)/shard_map/all_to_all | solution.py:47
  135.0 28.0 %all-to-all-done = f32[64,1,4096]{2,1,0:T(1,128)S(1)} async-done(((f32[64,1,4096]{2,1,0:T(1,128)}), f32[64,1,4096]{2,1,0:T(1,128)S(1)}, u32[]{:S(2)}, u32[]{:S(2)}) %all-to-all-start) | async-done | bytes 1048608 | tf_op jit(solution)/shard_map/all_to_all | solution.py:47
  163.0 0.9 reduce_sum.188
  163.9 2.5 fusion.10
  166.4 1.5 add_convert_fusion
  167.9 2.4 copy.23
  170.3 4.8 %all-to-all-start.2 = ((bf16[4,16,32,1024]{3,2,1,0:T(8,128)(2,1)}), bf16[4,16,32,1024]{3,2,1,0:T(8,128)(2,1)}, u32[]{:S(2)}, u32[]{:S(2)}) async-start(bf16[4,16,32,1024]{3,2,1,0:T(8,128)(2,1)} %bitcast.27), calls=%async_computation.2 | async-start | bytes 8388608 | tf_op jit(solution)/shard_map/all_to_all | solution.py:70
  175.2 0.6 fusion.3
  175.8 3.3 %convolution_convert_fusion.1 = bf16[4,32,1024]{2,1,0:T(8,128)(2,1)S(1)} fusion(bf16[4,32,2048]{2,1,0:T(8,128)(2,1)S(1)} %bitcast.31, bf16[2048,1024,1]{1,0,2:T(8,128)(2,1)} %bitcast.25), kind=kOutput, calls=%fused_computation.11 | convolution fusion | flops 537001984 | bytes 4980736 | tf_op jit(solution)/shard_map/dot_general | solution.py:106
  179.1 0.7 convolution_convert_fusion
  179.8 0.9 pad_maximum_fusion
  180.7 42.2 %all-to-all-done.2 = bf16[4,16,32,1024]{3,2,1,0:T(8,128)(2,1)} async-done(((bf16[4,16,32,1024]{3,2,1,0:T(8,128)(2,1)}), bf16[4,16,32,1024]{3,2,1,0:T(8,128)(2,1)}, u32[]{:S(2)}, u32[]{:S(2)}) %all-to-all-start.2) | async-done | bytes 4194336 | tf_op jit(solution)/shard_map/all_to_all | solution.py:70
  222.8 5.5 %all-to-all-start.4 = ((bf16[4,32,2048]{2,1,0:T(8,128)(2,1)}), bf16[4,32,2048]{2,1,0:T(8,128)(2,1)S(1)}, u32[]{:S(2)}, u32[]{:S(2)}) async-start(bf16[4,32,2048]{2,1,0:T(8,128)(2,1)} %pad_maximum_fusion), calls=%async_computation.4 | async-start | bytes 1048576 | tf_op jit(solution)/shard_map/all_to_all | solution.py:70
  228.3 4.4 %reduce_sum.192 = bf16[16,32,1024]{2,1,0:T(8,128)(2,1)} reduce(bf16[4,16,32,1024]{3,2,1,0:T(8,128)(2,1)} %all-to-all-done.2, bf16[]{:T(256)} %constant.102.clone.1), dimensions={0}, to_apply=%region_9.10 | reduce | flops 1572864 | bytes 5242882 | tf_op jit(solution)/shard_map/reduce_sum | solution.py:71
  232.7 2.7 all-to-all-done.4
  235.5 7.1 %all-to-all-start.3 = ((bf16[16,32,1024]{2,1,0:T(8,128)(2,1)}), bf16[16,32,1024]{2,1,0:T(8,128)(2,1)S(1)}, u32[]{:S(2)}, u32[]{:S(2)}) async-start(bf16[16,32,1024]{2,1,0:T(8,128)(2,1)} %reduce_sum.192), calls=%async_computation.3 | async-start | bytes 2097152 | tf_op jit(solution)/shard_map/all_to_all | solution.py:78
  243.2 0.7 log_reduce_fusion.1
  243.9 0.7 log_reduce_fusion
  244.5 0.7 log_reduce_fusion.3
  245.2 0.7 log_reduce_fusion.2
  248.5 5.5 %psum.35 = f32[]{:T(128)} all-reduce(f32[]{:T(128)S(6)} %sub.53), channel_id=1, replica_groups=mesh['row_0'=2,'row_1'=2,'col_0'=8,'col_1'=2,'col_2'=4] {'row_0'}, use_global_device_ids=true, to_apply=%region_20.21 | all-reduce | flops 1 | bytes 8 | tf_op jit(solution)/shard_map/psum | solution.py:85
  254.0 3.1 %psum.36 = f32[]{:T(128)} all-reduce(f32[]{:T(128)} %psum.35), channel_id=1, replica_groups=mesh['row_0'=2,'row_1'=2,'col_0'=8,'col_1'=2,'col_2'=4] {'row_1'}, use_global_device_ids=true, to_apply=%region_21.22 | all-reduce | flops 1 | bytes 8 | tf_op jit(solution)/shard_map/psum | solution.py:85
  257.0 20.9 %psum.37 = f32[]{:T(128)} all-reduce(f32[]{:T(128)} %psum.36), channel_id=1, replica_groups=mesh['row_0'=2,'row_1'=2,'col_0'=8,'col_1'=2,'col_2'=4] {'col_0'}, use_global_device_ids=true, to_apply=%region_22.23 | all-reduce | flops 1 | bytes 8 | tf_op jit(solution)/shard_map/psum | solution.py:85
  277.9 7.1 %psum.38 = f32[]{:T(128)} all-reduce(f32[]{:T(128)} %psum.37), channel_id=1, replica_groups=mesh['row_0'=2,'row_1'=2,'col_0'=8,'col_1'=2,'col_2'=4] {'col_1'}, use_global_device_ids=true, to_apply=%region_23.24 | all-reduce | flops 1 | bytes 8 | tf_op jit(solution)/shard_map/psum | solution.py:85
  285.0 9.5 %psum.39 = f32[]{:T(128)} all-reduce(f32[]{:T(128)} %psum.38), channel_id=1, replica_groups=mesh['row_0'=2,'row_1'=2,'col_0'=8,'col_1'=2,'col_2'=4] {'col_2'}, use_global_device_ids=true, to_apply=%region_24.25 | all-reduce | flops 1 | bytes 8 | tf_op jit(solution)/shard_map/psum | solution.py:85
  295.1 0.1 convert_reduce_fusion.1
  295.3 0.2 multiply_reduce_fusion
  295.5 0.8 subtract_divide_fusion
  296.3 0.2 convert_reduce_fusion
  296.5 0.2 multiply_reduce_fusion.2
  296.7 0.8 subtract_divide_fusion.2
  (30 shorter events, 0.2 us)
Async XLA Ops:
  7.2 49.8 %all-gather.4.cloned.1.call-start = ((), (), s32[]{:S(2)}) async-start(), calls=%async_computation.5 | async-start | bytes 1179648 | tf_op jit(solution)/shard_map/all_gather | solution.py:25
  15.7 92.2 %all-gather.6.cloned.1.call-start = ((), (), s32[]{:S(2)}) async-start(), calls=%async_computation.6 | async-start | bytes 5242880 | tf_op jit(solution)/shard_map/all_gather | solution.py:25
  66.5 45.6 %copy-start.2 = (bf16[128,2048]{1,0:T(8,128)(2,1)}, bf16[128,2048]{1,0:T(8,128)(2,1)S(1)}, u32[]{:S(2)}) copy-start(bf16[128,2048]{1,0:T(8,128)(2,1)S(1)} %all_gather.15) | copy-start | bytes 1572868
  110.5 4.0 %copy-start = (bf16[8,2,4,32,1024]{4,3,2,1,0:T(8,128)(2,1)}, bf16[8,2,4,32,1024]{4,3,2,1,0:T(8,128)(2,1)S(1)}, u32[]{:S(2)}) copy-start(bf16[8,2,4,32,1024]{4,3,2,1,0:T(8,128)(2,1)S(1)} %copy.12) | copy-start | bytes 12582916
  115.1 5.8 %all-to-all-start.1 = ((f32[4,1,256]{2,1,0:T(1,128)}), f32[4,1,256]{2,1,0:T(1,128)S(1)}, u32[]{:S(2)}, u32[]{:S(2)}) async-start(f32[4,1,256]{2,1,0:T(1,128)} %broadcast_in_dim.37), calls=%async_computation.1 | async-start | bytes 8192 | tf_op jit(solution)/shard_map/all_to_all | solution.py:47
  123.0 40.0 %all-to-all-start = ((f32[64,1,4096]{2,1,0:T(1,128)}), f32[64,1,4096]{2,1,0:T(1,128)S(1)}, u32[]{:S(2)}, u32[]{:S(2)}) async-start(f32[64,1,4096]{2,1,0:T(1,128)} %broadcast_in_dim.36), calls=%async_computation | async-start | bytes 2097152 | tf_op jit(solution)/shard_map/all_to_all | solution.py:47
  163.9 2.5 copy-start.3
  170.3 52.5 %all-to-all-start.2 = ((bf16[4,16,32,1024]{3,2,1,0:T(8,128)(2,1)}), bf16[4,16,32,1024]{3,2,1,0:T(8,128)(2,1)}, u32[]{:S(2)}, u32[]{:S(2)}) async-start(bf16[4,16,32,1024]{3,2,1,0:T(8,128)(2,1)} %bitcast.27), calls=%async_computation.2 | async-start | bytes 8388608 | tf_op jit(solution)/shard_map/all_to_all | solution.py:70
  175.2 3.9 %copy-start.1 = (bf16[8,2,4,32,1024]{4,3,2,1,0:T(8,128)(2,1)S(1)}, bf16[8,2,4,32,1024]{4,3,2,1,0:T(8,128)(2,1)}, u32[]{:S(2)}) copy-start(bf16[8,2,4,32,1024]{4,3,2,1,0:T(8,128)(2,1)} %copy-done) | copy-start | bytes 12582916
  222.8 12.6 %all-to-all-start.4 = ((bf16[4,32,2048]{2,1,0:T(8,128)(2,1)}), bf16[4,32,2048]{2,1,0:T(8,128)(2,1)S(1)}, u32[]{:S(2)}, u32[]{:S(2)}) async-start(bf16[4,32,2048]{2,1,0:T(8,128)(2,1)} %pad_maximum_fusion), calls=%async_computation.4 | async-start | bytes 1048576 | tf_op jit(solution)/shard_map/all_to_all | solution.py:70
  228.3 67.0 %copy-start.5 = (bf16[32,1024]{1,0:T(8,128)(2,1)S(1)}, bf16[32,1024]{1,0:T(8,128)(2,1)}, u32[]{:S(2)}) copy-start(bf16[32,1024]{1,0:T(8,128)(2,1)} %param.4) | copy-start | bytes 196612
  228.3 67.0 %copy-start.6 = (bf16[32,1024]{1,0:T(8,128)(2,1)S(1)}, bf16[32,1024]{1,0:T(8,128)(2,1)}, u32[]{:S(2)}) copy-start(bf16[32,1024]{1,0:T(8,128)(2,1)} %param.5) | copy-start | bytes 196612
  228.3 68.2 %copy-start.4 = (bf16[32,1024]{1,0:T(8,128)(2,1)S(1)}, bf16[32,1024]{1,0:T(8,128)(2,1)}, u32[]{:S(2)}) copy-start(bf16[32,1024]{1,0:T(8,128)(2,1)} %param.3) | copy-start | bytes 196612
  235.5 60.9 %all-to-all-start.3 = ((bf16[16,32,1024]{2,1,0:T(8,128)(2,1)}), bf16[16,32,1024]{2,1,0:T(8,128)(2,1)S(1)}, u32[]{:S(2)}, u32[]{:S(2)}) async-start(bf16[16,32,1024]{2,1,0:T(8,128)(2,1)} %reduce_sum.192), calls=%async_computation.3 | async-start | bytes 2097152 | tf_op jit(solution)/shard_map/all_to_all | solution.py:78
Sparse Core Ops, SparseCore 0:
  15.8 41.1 all-gather.3
  58.8 49.1 all-gather.5
where the time goes:
time: 306 us; the launch traced here: 305 us
  waiting for transfers between devices  157 us (51%)
  blocking collectives  59.1 us (19%)
  starting transfers between devices  33.5 us (11%)
  between operations  19.3 us (6%)
  other arithmetic  16.6 us (5%)
  matrix products  11.9 us (4%)
  local copies, waits for them, and re-layouts  7.67 us (3%)
    all_gather x2, waiting for transfers between devices, stacked_from(): parts = lax.all_gather(parts, axes[k], axis=0, tiled=True)  82.7 us
    psum x5, blocking collectives, over_axes(): return functools.reduce(lax.psum, axes, array)  46 us
    all_to_all x2, waiting for transfers between devices, summed_on_arrival(): parts = lax.all_to_all(split_up(array, dim, peers), axis, 0, 0, tiled=True)  44.9 us
    all_to_all x2, waiting for transfers between devices, copy_for_each(): return lax.all_to_all(copies, axis, split_axis=0, concat_axis=0, tiled=True)  29.7 us
    all_to_all x2, starting transfers between devices, copy_for_each(): return lax.all_to_all(copies, axis, split_axis=0, concat_axis=0, tiled=True)  16.1 us
    all_to_all x2, starting transfers between devices, summed_on_arrival(): parts = lax.all_to_all(split_up(array, dim, peers), axis, 0, 0, tiled=True)  10.3 us
    all_to_all x1, starting transfers between devices, sum_by_axis(): lax.all_to_all(nearer.astype(jnp.bfloat16), far, split_axis=0, concat_axi...  7.08 us
    all_gather x1, blocking collectives, stacked_from(): parts = lax.all_gather(parts, axes[k], axis=0, tiled=True)  6.54 us
  transfers between devices with their start and end apart: 7, of which 6 were waited for; matrix products, arithmetic and copies ran while one was open for 5% of the time, Pallas kernels for 0%

commit v1 on v0

--- a/solution.py
+++ b/solution.py
@@ -22,7 +22,8 @@
 def stacked_from(array, axes, sequence):
     parts = array[None]
     for k in sequence:
-        parts = lax.all_gather(parts, axes[k], axis=0, tiled=True)
+        outgoing = jnp.stack([parts] * lax.axis_size(axes[k]))
+        parts = jnp.concatenate(lax.all_to_all(outgoing, axes[k], 0, 0), axis=0)
     carried = [lax.axis_size(axes[k]) for k in reversed(sequence)]
     parts = parts.reshape(*carried, *array.shape)
     turned = sorted(range(len(sequence)), key=lambda place: sequence[len(sequence) - 1 - place])

time: 306 us -> 286 us (0.935)
  waiting for transfers between devices: 157 us -> 114 us
  blocking collectives: 59.1 us -> 95.5 us
  between operations: 19.3 us -> 5.91 us
    all_gather x2 -> x0, waiting for transfers between devices: 82.7 us -> none  [stacked_from(): parts = lax.all_gather(parts, axes[k], axis=0, tiled=True)]
    all_to_all x0 -> x2, blocking collectives: none -> 42.9 us  [stacked_from(): parts = jnp.concatenate(lax.all_to_all(outgoing, axes[k], 0, 0), axis=0)]
    all_to_all x0 -> x1, waiting for transfers between devices: none -> 39.1 us  [stacked_from(): parts = jnp.concatenate(lax.all_to_all(outgoing, axes[k], 0, 0), axis=0)]
    all_gather x1 -> x0, blocking collectives: 6.54 us -> none  [stacked_from(): parts = lax.all_gather(parts, axes[k], axis=0, tiled=True)]
    another operation x0 -> x3, local copies, waits for them, and re-layouts: none -> 5.33 us  [the longest x2 2.7 us: stacked_from(): outgoing = jnp.stack([parts] * lax.axis_size(axes[k]))]
    all_to_all x0 -> x1, starting transfers between devices: none -> 4.99 us  [stacked_from(): parts = jnp.concatenate(lax.all_to_all(outgoing, axes[k], 0, 0), axis=0)]
    all_to_all x2, starting transfers between devices: 16.1 us -> 12.3 us  [copy_for_each(): return lax.all_to_all(copies, axis, split_axis=0, concat_axis=0, tiled=True)]
  transfers between devices with their start and end apart: 7 -> 6, of which waited for: 6 -> 5; matrix products, arithmetic and copies ran while one was open for 5% -> 5% of each run, Pallas kernels for 0% -> 0%
where the time goes in v1:
time: 286 us; the launch traced here: 285 us
  waiting for transfers between devices  114 us (40%)
  blocking collectives  95.5 us (33%)
  starting transfers between devices  34.1 us (12%)
  other arithmetic  14.1 us (5%)
  matrix products  11.9 us (4%)
  local copies, waits for them, and re-layouts  10.4 us (4%)
  between operations  5.91 us (2%)
    psum x5, blocking collectives, over_axes(): return functools.reduce(lax.psum, axes, array)  46.1 us
    all_to_all x2, waiting for transfers between devices, summed_on_arrival(): parts = lax.all_to_all(split_up(array, dim, peers), axis, 0, 0, tiled=True)  44.7 us
    all_to_all x2, blocking collectives, stacked_from(): parts = jnp.concatenate(lax.all_to_all(outgoing, axes[k], 0, 0), axis=0)  42.9 us
    all_to_all x1, waiting for transfers between devices, stacked_from(): parts = jnp.concatenate(lax.all_to_all(outgoing, axes[k], 0, 0), axis=0)  39.1 us
    all_to_all x2, waiting for transfers between devices, copy_for_each(): return lax.all_to_all(copies, axis, split_axis=0, concat_axis=0, tiled=True)  29.7 us
    all_to_all x2, starting transfers between devices, copy_for_each(): return lax.all_to_all(copies, axis, split_axis=0, concat_axis=0, tiled=True)  12.3 us
    all_to_all x2, starting transfers between devices, summed_on_arrival(): parts = lax.all_to_all(split_up(array, dim, peers), axis, 0, 0, tiled=True)  9.69 us
    all_to_all x1, starting transfers between devices, sum_by_axis(): lax.all_to_all(nearer.astype(jnp.bfloat16), far, split_axis=0, concat_axi...  7.07 us
  transfers between devices with their start and end apart: 6, of which 5 were waited for; matrix products, arithmetic and copies ran while one was open for 5% of the time, Pallas kernels for 0%

profile of v1, /device:TPU:24, one launch (start us, length us, event | category | flops | bytes accessed | tf_op | source)
XLA Modules:
  0.0 285.4 jit_solution(13658419012430485261)
XLA Ops:
  0.6 1.0 fusion.24
  1.6 0.9 convert_bitcast_fusion
  2.6 7.0 %all_to_all.42 = bf16[2,1,32,1024]{3,2,1,0:T(8,128)(2,1)S(1)} all-to-all(bf16[2,1,32,1024]{3,2,1,0:T(8,128)(2,1)S(1)} %pad_maximum_fusion.1), channel_id=1, replica_groups=mesh['row_0'=2,'row_1'=2,'col_0'=8,'col_1'=2,'col_2'=4] {'col_1'}, dimensions={0} | all-to-all | bytes 262144 | tf_op jit(solution)/shard_map/all_to_all | solution.py:26
  9.6 0.1 stack.10
  9.7 35.8 %all_to_all.43 = bf16[8,2,32,1024]{3,2,1,0:T(8,128)(2,1)S(1)} all-to-all(bf16[8,2,32,1024]{3,2,1,0:T(8,128)(2,1)S(1)} %stack.10), channel_id=1, replica_groups=mesh['row_0'=2,'row_1'=2,'col_0'=8,'col_1'=2,'col_2'=4] {'col_0'}, dimensions={0} | all-to-all | bytes 2097152 | tf_op jit(solution)/shard_map/all_to_all | solution.py:26
  45.6 2.6 stack.11
  48.2 5.0 %all-to-all-start.2 = ((bf16[4,16,32,1024]{3,2,1,0:T(8,128)(2,1)}), bf16[4,16,32,1024]{3,2,1,0:T(8,128)(2,1)}, u32[]{:S(2)}, u32[]{:S(2)}) async-start(bf16[4,16,32,1024]{3,2,1,0:T(8,128)(2,1)} %stack.11), calls=%async_computation.2 | async-start | bytes 8388608 | tf_op jit(solution)/shard_map/all_to_all | solution.py:26
  53.2 0.1 fusion.25
  53.3 0.1 fusion.26
  53.6 6.5 %all_gather.3 = bf16[128,2048]{1,0:T(8,128)(2,1)S(1)} all-gather(bf16[32,2048]{1,0:T(8,128)(2,1)S(1)} %pad_maximum_fusion.2), channel_id=1, replica_groups=mesh['row_0'=2,'row_1'=2,'col_0'=8,'col_1'=2,'col_2'=4] {'row_0','row_1'}, dimensions={0}, use_global_device_ids=true | all-gather | bytes 655360 | tf_op jit(solution)/shard_map/all_gather | solution.py:43
  60.1 39.1 %all-to-all-done.2 = bf16[4,16,32,1024]{3,2,1,0:T(8,128)(2,1)} async-done(((bf16[4,16,32,1024]{3,2,1,0:T(8,128)(2,1)}), bf16[4,16,32,1024]{3,2,1,0:T(8,128)(2,1)}, u32[]{:S(2)}, u32[]{:S(2)}) %all-to-all-start.2) | async-done | bytes 4194336 | tf_op jit(solution)/shard_map/all_to_all | solution.py:26
  99.2 2.6 copy.11
  101.8 1.5 convolution_multiply_fusion
  103.4 2.4 fusion
  105.8 0.6 broadcast_in_dim.19
  106.4 4.0 %all-to-all-start.4 = ((f32[4,1,256]{2,1,0:T(1,128)}), f32[4,1,256]{2,1,0:T(1,128)S(1)}, u32[]{:S(2)}, u32[]{:S(2)}) async-start(f32[4,1,256]{2,1,0:T(1,128)} %broadcast_in_dim.19), calls=%async_computation.4 | async-start | bytes 8192 | tf_op jit(solution)/shard_map/all_to_all | solution.py:48
  110.4 1.8 all-to-all-done.4
  112.2 2.0 broadcast_in_dim.18
  114.1 8.4 %all-to-all-start.3 = ((f32[64,1,4096]{2,1,0:T(1,128)}), f32[64,1,4096]{2,1,0:T(1,128)S(1)}, u32[]{:S(2)}, u32[]{:S(2)}) async-start(f32[64,1,4096]{2,1,0:T(1,128)} %broadcast_in_dim.18), calls=%async_computation.3 | async-start | bytes 2097152 | tf_op jit(solution)/shard_map/all_to_all | solution.py:48
  122.6 28.0 %all-to-all-done.3 = f32[64,1,4096]{2,1,0:T(1,128)S(1)} async-done(((f32[64,1,4096]{2,1,0:T(1,128)}), f32[64,1,4096]{2,1,0:T(1,128)S(1)}, u32[]{:S(2)}, u32[]{:S(2)}) %all-to-all-start.3) | async-done | bytes 1048608 | tf_op jit(solution)/shard_map/all_to_all | solution.py:48
  150.5 0.9 reduce_sum.188
  151.4 2.5 fusion.10
  153.9 1.5 add_convert_fusion
  155.4 2.4 copy.22
  157.8 5.0 %all-to-all-start.5 = ((bf16[4,16,32,1024]{3,2,1,0:T(8,128)(2,1)}), bf16[4,16,32,1024]{3,2,1,0:T(8,128)(2,1)}, u32[]{:S(2)}, u32[]{:S(2)}) async-start(bf16[4,16,32,1024]{3,2,1,0:T(8,128)(2,1)} %bitcast.30), calls=%async_computation.5 | async-start | bytes 8388608 | tf_op jit(solution)/shard_map/all_to_all | solution.py:71
  162.9 0.6 fusion.3
  163.5 3.3 %convolution_convert_fusion.1 = bf16[4,32,1024]{2,1,0:T(8,128)(2,1)S(1)} fusion(bf16[4,32,2048]{2,1,0:T(8,128)(2,1)S(1)} %bitcast.34, bf16[2048,1024,1]{1,0,2:T(8,128)(2,1)} %bitcast.28), kind=kOutput, calls=%fused_computation.11 | convolution fusion | flops 537001984 | bytes 4980736 | tf_op jit(solution)/shard_map/dot_general | solution.py:107
  166.8 0.7 convolution_convert_fusion
  167.5 0.9 pad_maximum_fusion
  168.4 42.0 %all-to-all-done.5 = bf16[4,16,32,1024]{3,2,1,0:T(8,128)(2,1)} async-done(((bf16[4,16,32,1024]{3,2,1,0:T(8,128)(2,1)}), bf16[4,16,32,1024]{3,2,1,0:T(8,128)(2,1)}, u32[]{:S(2)}, u32[]{:S(2)}) %all-to-all-start.5) | async-done | bytes 4194336 | tf_op jit(solution)/shard_map/all_to_all | solution.py:71
  210.4 4.7 %all-to-all-start.7 = ((bf16[4,32,2048]{2,1,0:T(8,128)(2,1)}), bf16[4,32,2048]{2,1,0:T(8,128)(2,1)S(1)}, u32[]{:S(2)}, u32[]{:S(2)}) async-start(bf16[4,32,2048]{2,1,0:T(8,128)(2,1)} %pad_maximum_fusion), calls=%async_computation.7 | async-start | bytes 1048576 | tf_op jit(solution)/shard_map/all_to_all | solution.py:71
  215.0 4.4 %reduce_sum.192 = bf16[16,32,1024]{2,1,0:T(8,128)(2,1)} reduce(bf16[4,16,32,1024]{3,2,1,0:T(8,128)(2,1)} %all-to-all-done.5, bf16[]{:T(256)} %constant.102.clone.1), dimensions={0}, to_apply=%region_9.10 | reduce | flops 1572864 | bytes 5242882 | tf_op jit(solution)/shard_map/reduce_sum | solution.py:72
  219.5 2.8 all-to-all-done.7
  222.2 7.1 %all-to-all-start.6 = ((bf16[16,32,1024]{2,1,0:T(8,128)(2,1)}), bf16[16,32,1024]{2,1,0:T(8,128)(2,1)S(1)}, u32[]{:S(2)}, u32[]{:S(2)}) async-start(bf16[16,32,1024]{2,1,0:T(8,128)(2,1)} %reduce_sum.192), calls=%async_computation.6 | async-start | bytes 2097152 | tf_op jit(solution)/shard_map/all_to_all | solution.py:79
  229.9 0.7 log_reduce_fusion.1
  230.6 0.7 log_reduce_fusion
  231.3 0.7 log_reduce_fusion.3
  232.0 0.7 log_reduce_fusion.2
  235.2 5.5 %psum.35 = f32[]{:T(128)} all-reduce(f32[]{:T(128)S(6)} %sub.53), channel_id=1, replica_groups=mesh['row_0'=2,'row_1'=2,'col_0'=8,'col_1'=2,'col_2'=4] {'row_0'}, use_global_device_ids=true, to_apply=%region_20.21 | all-reduce | flops 1 | bytes 8 | tf_op jit(solution)/shard_map/psum | solution.py:86
  240.7 3.1 %psum.36 = f32[]{:T(128)} all-reduce(f32[]{:T(128)} %psum.35), channel_id=1, replica_groups=mesh['row_0'=2,'row_1'=2,'col_0'=8,'col_1'=2,'col_2'=4] {'row_1'}, use_global_device_ids=true, to_apply=%region_21.22 | all-reduce | flops 1 | bytes 8 | tf_op jit(solution)/shard_map/psum | solution.py:86
  243.8 20.9 %psum.37 = f32[]{:T(128)} all-reduce(f32[]{:T(128)} %psum.36), channel_id=1, replica_groups=mesh['row_0'=2,'row_1'=2,'col_0'=8,'col_1'=2,'col_2'=4] {'col_0'}, use_global_device_ids=true, to_apply=%region_22.23 | all-reduce | flops 1 | bytes 8 | tf_op jit(solution)/shard_map/psum | solution.py:86
  264.7 7.1 %psum.38 = f32[]{:T(128)} all-reduce(f32[]{:T(128)} %psum.37), channel_id=1, replica_groups=mesh['row_0'=2,'row_1'=2,'col_0'=8,'col_1'=2,'col_2'=4] {'col_1'}, use_global_device_ids=true, to_apply=%region_23.24 | all-reduce | flops 1 | bytes 8 | tf_op jit(solution)/shard_map/psum | solution.py:86
  271.7 9.6 %psum.39 = f32[]{:T(128)} all-reduce(f32[]{:T(128)} %psum.38), channel_id=1, replica_groups=mesh['row_0'=2,'row_1'=2,'col_0'=8,'col_1'=2,'col_2'=4] {'col_2'}, use_global_device_ids=true, to_apply=%region_24.25 | all-reduce | flops 1 | bytes 8 | tf_op jit(solution)/shard_map/psum | solution.py:86
  282.1 0.2 multiply_reduce_fusion
  282.3 0.8 subtract_divide_fusion
  283.1 0.2 convert_reduce_fusion
  283.3 0.2 multiply_reduce_fusion.2
  283.5 0.8 subtract_divide_fusion.2
  (30 shorter events, 0.3 us)
Async XLA Ops:
  48.2 5.0 %copy-start.5 = (bf16[32,1024]{1,0:T(8,128)(2,1)S(1)}, bf16[32,1024]{1,0:T(8,128)(2,1)}, u32[]{:S(2)}) copy-start(bf16[32,1024]{1,0:T(8,128)(2,1)} %param.4) | copy-start | bytes 196612
  48.2 5.2 %copy-start.6 = (bf16[32,1024]{1,0:T(8,128)(2,1)S(1)}, bf16[32,1024]{1,0:T(8,128)(2,1)}, u32[]{:S(2)}) copy-start(bf16[32,1024]{1,0:T(8,128)(2,1)} %param.5) | copy-start | bytes 196612
  48.2 51.0 %all-to-all-start.2 = ((bf16[4,16,32,1024]{3,2,1,0:T(8,128)(2,1)}), bf16[4,16,32,1024]{3,2,1,0:T(8,128)(2,1)}, u32[]{:S(2)}, u32[]{:S(2)}) async-start(bf16[4,16,32,1024]{3,2,1,0:T(8,128)(2,1)} %stack.11), calls=%async_computation.2 | async-start | bytes 8388608 | tf_op jit(solution)/shard_map/all_to_all | solution.py:26
  60.1 43.2 %copy-start.2 = (bf16[128,2048]{1,0:T(8,128)(2,1)}, bf16[128,2048]{1,0:T(8,128)(2,1)S(1)}, u32[]{:S(2)}) copy-start(bf16[128,2048]{1,0:T(8,128)(2,1)S(1)} %all_gather.3) | copy-start | bytes 1572868
  101.8 4.0 %copy-start = (bf16[4,8,2,32,1024]{4,3,0,2,1:T(8,128)(2,1)}, bf16[4,8,2,32,1024]{4,3,0,2,1:T(8,128)(2,1)S(1)}, u32[]{:S(2)}) copy-start(bf16[4,8,2,32,1024]{4,3,0,2,1:T(8,128)(2,1)S(1)} %copy.11) | copy-start | bytes 12582916
  106.4 5.8 %all-to-all-start.4 = ((f32[4,1,256]{2,1,0:T(1,128)}), f32[4,1,256]{2,1,0:T(1,128)S(1)}, u32[]{:S(2)}, u32[]{:S(2)}) async-start(f32[4,1,256]{2,1,0:T(1,128)} %broadcast_in_dim.19), calls=%async_computation.4 | async-start | bytes 8192 | tf_op jit(solution)/shard_map/all_to_all | solution.py:48
  114.1 36.4 %all-to-all-start.3 = ((f32[64,1,4096]{2,1,0:T(1,128)}), f32[64,1,4096]{2,1,0:T(1,128)S(1)}, u32[]{:S(2)}, u32[]{:S(2)}) async-start(f32[64,1,4096]{2,1,0:T(1,128)} %broadcast_in_dim.18), calls=%async_computation.3 | async-start | bytes 2097152 | tf_op jit(solution)/shard_map/all_to_all | solution.py:48
  151.4 2.5 copy-start.3
  157.8 52.5 %all-to-all-start.5 = ((bf16[4,16,32,1024]{3,2,1,0:T(8,128)(2,1)}), bf16[4,16,32,1024]{3,2,1,0:T(8,128)(2,1)}, u32[]{:S(2)}, u32[]{:S(2)}) async-start(bf16[4,16,32,1024]{3,2,1,0:T(8,128)(2,1)} %bitcast.30), calls=%async_computation.5 | async-start | bytes 8388608 | tf_op jit(solution)/shard_map/all_to_all | solution.py:71
  162.9 3.9 %copy-start.1 = (bf16[4,8,2,32,1024]{4,3,0,2,1:T(8,128)(2,1)S(1)}, bf16[4,8,2,32,1024]{4,3,0,2,1:T(8,128)(2,1)}, u32[]{:S(2)}) copy-start(bf16[4,8,2,32,1024]{4,3,0,2,1:T(8,128)(2,1)} %copy-done) | copy-start | bytes 12582916
  210.4 11.9 %all-to-all-start.7 = ((bf16[4,32,2048]{2,1,0:T(8,128)(2,1)}), bf16[4,32,2048]{2,1,0:T(8,128)(2,1)S(1)}, u32[]{:S(2)}, u32[]{:S(2)}) async-start(bf16[4,32,2048]{2,1,0:T(8,128)(2,1)} %pad_maximum_fusion), calls=%async_computation.7 | async-start | bytes 1048576 | tf_op jit(solution)/shard_map/all_to_all | solution.py:71
  215.0 68.3 %copy-start.4 = (bf16[32,1024]{1,0:T(8,128)(2,1)S(1)}, bf16[32,1024]{1,0:T(8,128)(2,1)}, u32[]{:S(2)}) copy-start(bf16[32,1024]{1,0:T(8,128)(2,1)} %param.3) | copy-start | bytes 196612
  222.2 60.9 %all-to-all-start.6 = ((bf16[16,32,1024]{2,1,0:T(8,128)(2,1)}), bf16[16,32,1024]{2,1,0:T(8,128)(2,1)S(1)}, u32[]{:S(2)}, u32[]{:S(2)}) async-start(bf16[16,32,1024]{2,1,0:T(8,128)(2,1)} %reduce_sum.192), calls=%async_computation.6 | async-start | bytes 2097152 | tf_op jit(solution)/shard_map/all_to_all | solution.py:79
